TPU v7x, 32 devices: a whole 2x2x4 slice. The times are simulated.
32 devices in a mesh: rep: 2 (over y), seq: 8 (over z, x), head: 2 (over core).
Axes of the slice: x: 2, y: 2, z: 4, core: 2. Of those that a mesh axis runs over, the one named last changes fastest.
Arguments:
- prompt_query: bfloat16 [2048, 1792], P(('rep', 'seq', 'head')), parts along dimension 0, may hold values from -12 to 12
- prompt_key: bfloat16 [2048, 256], P(('rep', 'seq', 'head')), parts along dimension 0, may hold values from -12 to 12
- prompt_value: bfloat16 [2048, 256], P(('rep', 'seq', 'head')), parts along dimension 0, may hold values from -24 to 24
- prompt_length: int32 [2], P('rep'), parts along dimension 0, may hold values from 512 to 1024
- span_order: int32 [32], P('rep'), parts along dimension 0, may hold values from 0 to 15, each once
- new_query: bfloat16 [32, 1792], P('rep', 'head'), parts along dimension 0, may hold values from -12 to 12
- new_key: bfloat16 [32, 256], P('rep', 'head'), parts along dimension 0, may hold values from -12 to 12
- new_value: bfloat16 [32, 256], P('rep', 'head'), parts along dimension 0, may hold values from -24 to 24
- cache_key: bfloat16 [32, 2, 2048, 128], P('rep', 'head', 'seq'), parts along dimension 0, may hold values from -12 to 12
- cache_value: bfloat16 [32, 2, 2048, 128], P('rep', 'head', 'seq'), parts along dimension 0, may hold values from -24 to 24
- cache_length: int32 [32], P('rep'), parts along dimension 0, may hold values from 1280 to 2048
Outputs:
- prompt_attended: bfloat16 [2048, 1792], P(('rep', 'seq', 'head')), parts along dimension 0
- decode_attended: bfloat16 [32, 1792], P('rep', 'head'), parts along dimension 0
There are 2 independent parts, one for each index of `rep`. A program takes and returns all parts, laid end to end along the dimension named above; each array names one. Nothing has to cross between parts.
Inputs may be any that keep to these rules, and one draw needn't show every extreme that they name: `span_order`: each of the 16 spans stands once.
All inputs are finite; a program needn't handle non-finite values.
Results may differ from a plain program's by a relative error of at most 0.0045.
Values may be sent and summed in bfloat16 or wider, within the bound.
No kernel may reach another device: no remote copies, remote signals or barrier semaphores. Data moves between devices by JAX's collectives and lax.ppermute only.
A program may use at most 128 MiB of HBM per device.

v0:
```python
import functools
import math

import jax
import jax.numpy as jnp
from jax import lax
from jax.experimental import pallas as pl
from jax.experimental.pallas import tpu as pltpu
from jax.sharding import PartitionSpec as P

HD = 128
QH = 14
KVH = 2
NEG = -1e30
STAT = 3


def split3(x):
    hi = x.astype(jnp.bfloat16)
    rest = x - hi.astype(jnp.float32)
    mid = rest.astype(jnp.bfloat16)
    low = (rest - mid.astype(jnp.float32)).astype(jnp.bfloat16)
    return hi, mid, low


def join3(ref, at):
    return (
        ref[at].astype(jnp.float32) + ref[at + 1].astype(jnp.float32)
    ) + ref[at + 2].astype(jnp.float32)


def vmem(x):
    if x.size * x.dtype.itemsize > 1 << 20:
        return x
    return pltpu.with_memory_space_constraint(x, pltpu.VMEM)


def in_vmem():
    return pl.BlockSpec(memory_space=pltpu.VMEM)


def in_smem():
    return pl.BlockSpec(memory_space=pltpu.SMEM)


def decode_kernel(lens, q_ref, nk_ref, nv_ref, k_ref, v_ref, out_ref, q_scr, o_scr, l_scr, n_scr):
    step = pl.program_id(0)
    sessions, group, ctx = q_ref.shape[0], q_ref.shape[1] // HD, k_ref.shape[2]
    per_step = k_ref.shape[0]
    padded = q_scr.shape[0]
    scale = math.log2(math.e) / math.sqrt(HD)
    seq_id = lax.axis_index("seq")
    first = seq_id * ctx
    owner = jnp.full((1, 1), seq_id, jnp.int32) == 0

    @pl.when(step == 0)
    def _():
        n_scr[0] = nk_ref[...].astype(jnp.float32)
        n_scr[1] = nv_ref[...].astype(jnp.float32)
        for h in range(padded):
            if h < group:
                q_scr[h] = q_ref[:, h * HD : (h + 1) * HD].astype(jnp.float32)
            else:
                q_scr[h] = jnp.zeros((sessions, HD), jnp.float32)

    cols = lax.broadcasted_iota(jnp.int32, (padded, ctx), 1)
    scores, valids, owns, fresh = [], [], [], []
    for i in range(per_step):
        s = step * per_step + i
        q = q_scr[:, pl.ds(s, 1), :].reshape(padded, HD)
        scores.append(
            lax.dot_general(
                q.astype(jnp.bfloat16),
                k_ref[i, 0],
                (((1,), (1,)), ((), ())),
                preferred_element_type=jnp.float32,
            )
        )
        valids.append((cols < lens[s] - first).astype(jnp.float32))
        owns.append(q * n_scr[0, pl.ds(s, 1), :])
        fresh.append(jnp.broadcast_to(n_scr[1, pl.ds(s, 1), :], (padded, HD)))
    valid = jnp.concatenate(valids, axis=0) > 0.0
    score = jnp.where(valid, jnp.concatenate(scores, axis=0) * scale, NEG)
    own = jnp.sum(jnp.concatenate(owns, axis=0), axis=1, keepdims=True) * scale
    own = jnp.where(owner, own, NEG)
    top = jnp.maximum(jnp.max(score, axis=1, keepdims=True), own)
    weight = jnp.where(valid, jnp.exp2(score - top), 0.0)
    own_w = jnp.where(owner, jnp.exp2(own - top), 0.0)
    total = jnp.sum(weight, axis=1, keepdims=True) + own_w
    weight = weight.astype(jnp.bfloat16)
    acc = jnp.concatenate(
        [
            jnp.dot(
                weight[i * padded : (i + 1) * padded],
                v_ref[i, 0],
                preferred_element_type=jnp.float32,
            )
            for i in range(per_step)
        ],
        axis=0,
    )
    acc = acc + own_w.astype(jnp.bfloat16).astype(jnp.float32) * jnp.concatenate(fresh, axis=0)
    live = total > 0.0
    safe = jnp.where(live, total, 1.0)
    out = acc / safe
    lse = jnp.broadcast_to(jnp.where(live, top + jnp.log2(safe), NEG), out.shape)
    for i in range(per_step):
        s = step * per_step + i
        part = slice(i * padded, (i + 1) * padded)
        o_scr[:, pl.ds(s, 1), :] = out[part].reshape(padded, 1, HD)
        l_scr[:, pl.ds(s, 1), :] = lse[part].reshape(padded, 1, HD)

    @pl.when(step == pl.num_programs(0) - 1)
    def _():
        lane = lax.broadcasted_iota(jnp.int32, (sessions, HD), 1)
        stat = jnp.zeros((sessions, HD), jnp.float32)
        for h in range(group):
            out_ref[h] = o_scr[h].astype(jnp.bfloat16)
            stat = jnp.where(lane == h, l_scr[h], stat)
        for j, part in enumerate(split3(stat)):
            out_ref[group + j] = part


def decode_local(lens, query, new_key, new_value, cache_key, cache_value):
    sessions, width = query.shape
    group = width // HD
    ctx = cache_key.shape[2]
    per_step = max(n for n in (1, 2, 4) if sessions % n == 0)
    padded = -(-group // 8) * 8
    cache = pl.BlockSpec((per_step, 1, ctx, HD), lambda i: (i, 0, 0, 0))
    return pl.pallas_call(
        decode_kernel,
        grid=(sessions // per_step,),
        in_specs=[in_smem(), in_vmem(), in_vmem(), in_vmem(), cache, cache],
        out_specs=in_vmem(),
        scratch_shapes=[pltpu.VMEM((padded, sessions, HD), jnp.float32)] * 3
        + [pltpu.VMEM((2, sessions, HD), jnp.float32)],
        out_shape=pltpu.VMEM((group + STAT, sessions, HD), jnp.bfloat16),
        cost_estimate=pl.CostEstimate(
            flops=2_000_000_000, bytes_accessed=cache_key.size * 4, transcendentals=0
        ),
        name="decode_local",
    )(lens, vmem(query), vmem(new_key), vmem(new_value), cache_key, cache_value)


def merge_kernel(a_ref, b_ref, out_ref, *, final):
    group = a_ref.shape[0] - STAT
    la = join3(a_ref, group)
    lb = join3(b_ref, group)
    top = jnp.maximum(la, lb)
    ea = jnp.exp2(la - top)
    eb = jnp.exp2(lb - top)
    total = ea + eb
    wa = ea / total
    wb = eb / total
    for h in range(group):
        out = a_ref[h].astype(jnp.float32) * wa[:, h : h + 1] + b_ref[h].astype(
            jnp.float32
        ) * wb[:, h : h + 1]
        if final:
            out_ref[:, h * HD : (h + 1) * HD] = out.astype(jnp.bfloat16)
        else:
            out_ref[h] = out.astype(jnp.bfloat16)
    if not final:
        for j, part in enumerate(split3(top + jnp.log2(total))):
            out_ref[group + j] = part


def merge(a, b, final):
    rows, sessions, _ = a.shape
    shape = (sessions, (rows - STAT) * HD) if final else a.shape
    return pl.pallas_call(
        functools.partial(merge_kernel, final=final),
        in_specs=[in_vmem(), in_vmem()],
        out_specs=in_vmem(),
        out_shape=jax.ShapeDtypeStruct(shape, jnp.bfloat16)
        if final
        else pltpu.VMEM(shape, jnp.bfloat16),
        name="decode_merge",
    )(vmem(a), vmem(b))


def attend_kernel(span_ref, len_ref, q_ref, *refs, bases, bits, first, last):
    kv_refs, refs = refs[: len(bases)], refs[len(bases) :]
    if not first:
        state_in, refs = refs[:3], refs[3:]
    rows = q_ref.shape[0]
    group = QH // KVH
    scale = math.log2(math.e) / math.sqrt(HD)
    me = lax.axis_index("seq") * lax.axis_size("head") + lax.axis_index("head")
    length = len_ref[0]
    q_pos = span_ref[me] * rows + lax.broadcasted_iota(jnp.int32, (rows, 1), 0)
    limit = jnp.minimum(q_pos, length - 1)
    keys = kv_refs[0].shape[0]
    block = math.gcd(keys, 256)
    chunks = block // rows
    state = []
    for g in range(KVH):
        if first:
            shape = (group * rows, HD)
            state.append(
                (
                    jnp.zeros(shape, jnp.float32),
                    jnp.full((group * rows, 1), NEG, jnp.float32),
                    jnp.zeros((group * rows, 1), jnp.float32),
                )
            )
        else:
            state.append((state_in[0][g], state_in[1][g][:, :1], state_in[2][g][:, :1]))
    queries = [
        jnp.concatenate(
            [q_ref[:, (g * group + h) * HD : (g * group + h + 1) * HD] for h in range(group)], axis=0
        )
        for g in range(KVH)
    ]

    def positions(b, base):
        lane = lax.broadcasted_iota(jnp.int32, (1, block), 1)
        pos = lane
        for c in range(chunks):
            at = b * chunks + c
            source = me ^ base
            for t, bit in enumerate(bits):
                source = source ^ (((at >> t) & 1) * bit)
            start = (span_ref[source] - c) * rows
            inside = (lane >= c * rows) & (lane < (c + 1) * rows)
            pos = jnp.where(inside, lane + start, pos)
        return pos

    def advance(state, parts):
        allowed = jnp.concatenate(
            [(pos <= limit).astype(jnp.float32) for _, _, pos in parts], axis=1
        )
        allowed = jnp.concatenate([allowed] * group, axis=0) > 0.0
        result = []
        for g in range(KVH):
            acc, m_old, total = state[g]
            score = jnp.concatenate(
                [
                    lax.dot_general(
                        queries[g],
                        ref[at, g * HD : (g + 1) * HD],
                        (((1,), (1,)), ((), ())),
                        preferred_element_type=jnp.float32,
                    )
                    for ref, at, _ in parts
                ],
                axis=1,
            )
            score = jnp.where(allowed, score * scale, NEG)
            m_new = jnp.maximum(m_old, jnp.max(score, axis=1, keepdims=True))
            weight = jnp.where(allowed, jnp.exp2(score - m_new), 0.0)
            factor = jnp.exp2(m_old - m_new)
            total = total * factor + jnp.sum(weight, axis=1, keepdims=True)
            weight = weight.astype(jnp.bfloat16)
            acc = acc * factor
            for n, (ref, at, _) in enumerate(parts):
                acc = acc + jnp.dot(
                    weight[:, n * block : (n + 1) * block],
                    ref[at, (KVH + g) * HD : (KVH + g + 1) * HD],
                    preferred_element_type=jnp.float32,
                )
            result.append((acc, m_new, total))
        return result

    if keys == block:
        at = slice(0, block)
        state = advance(state, [(r, at, positions(0, base)) for r, base in zip(kv_refs, bases)])
    else:

        def body(b, state):
            at = pl.ds(pl.multiple_of(b * block, block), block)
            return advance(state, [(r, at, positions(b, base)) for r, base in zip(kv_refs, bases)])

        state = lax.fori_loop(0, keys // block, body, state)

    if last:
        live = q_pos < length
        for g in range(KVH):
            acc, _, total = state[g]
            out = acc / total
            for h in range(group):
                at = (g * group + h) * HD
                part = out[h * rows : (h + 1) * rows]
                refs[0][:, at : at + HD] = jnp.where(live, part, 0.0).astype(jnp.bfloat16)
    else:
        for g in range(KVH):
            for ref, value in zip(refs, state[g]):
                ref[g] = jnp.broadcast_to(value, ref.shape[1:])


def attend(spans, length, query, pieces, bases, bits, state, last):
    rows = query.shape[0]
    first = state is None
    shape = (KVH, QH // KVH * rows, HD)
    operands = [query, *pieces] + ([] if first else list(state))
    return pl.pallas_call(
        functools.partial(attend_kernel, bases=bases, bits=bits, first=first, last=last),
        in_specs=[in_smem(), in_smem()] + [in_vmem()] * len(operands),
        out_specs=in_vmem() if last else [in_vmem()] * 3,
        out_shape=jax.ShapeDtypeStruct(query.shape, jnp.bfloat16)
        if last
        else [pltpu.VMEM(shape, jnp.float32)] * 3,
        cost_estimate=pl.CostEstimate(
            flops=4_000_000_000, bytes_accessed=query.size * 2, transcendentals=0
        ),
        name="attend",
    )(spans, length, *(vmem(x) for x in operands[: 1 + len(pieces)]), *operands[1 + len(pieces) :])


def per_device(
    prompt_query,
    prompt_key,
    prompt_value,
    prompt_length,
    span_order,
    new_query,
    new_key,
    new_value,
    cache_key,
    cache_value,
    cache_length,
):
    seq, head = lax.axis_size("seq"), lax.axis_size("head")
    bits = [1 << b for b in reversed(range(seq.bit_length() - 1))]

    def swap(x, bit):
        return lax.ppermute(x, "seq", [(i, i ^ bit) for i in range(seq)])

    def partner(x):
        return lax.ppermute(x, "head", [(i, i ^ 1) for i in range(head)])

    kv = jnp.concatenate([prompt_key, prompt_value], axis=1)
    other = swap(kv, bits[0])
    dec = decode_local(
        cache_length, new_query, new_key, new_value, cache_key, cache_value
    )
    kv = jnp.concatenate([kv, other], axis=0)
    for bit in bits[1:-1]:
        other = swap(kv, bit)
        kv = jnp.concatenate([kv, other], axis=0)
    masks = [bit * head for bit in bits[:-1]]
    far = bits[-1] * head
    kv_far = swap(kv, bits[-1])
    kv_pair = partner(kv)
    state = attend(
        span_order, prompt_length, prompt_query, [kv, kv_pair], (0, 1), masks, None, False
    )
    kv_far_pair = partner(kv_far)
    prompt_attended = attend(
        span_order,
        prompt_length,
        prompt_query,
        [kv_far, kv_far_pair],
        (far, far ^ 1),
        masks,
        state,
        True,
    )

    order = bits[1:] + bits[:1]
    for n, bit in enumerate(order):
        other = swap(dec, bit)
        dec = merge(dec, other, n == len(order) - 1)
    return (prompt_attended, dec)


def solution(mesh):
    return jax.shard_map(
        per_device,
        mesh=mesh,
        in_specs=(
            P(("rep", "seq", "head"), None),
            P(("rep", "seq", "head"), None),
            P(("rep", "seq", "head"), None),
            P("rep"),
            P("rep"),
            P("rep", "head"),
            P("rep", "head"),
            P("rep", "head"),
            P("rep", "head", "seq", None),
            P("rep", "head", "seq", None),
            P("rep"),
        ),
        out_specs=(P(("rep", "seq", "head"), None), P("rep", "head")),
        check_vma=False,
    )
```

profile of v0, /device:TPU:0, one launch (start us, length us, event | category | flops | bytes accessed | tf_op | source)
XLA Modules:
  0.0 42.6 jit_solution(2425722914084815695)
XLA Ops:
  0.6 0.0 copy-start.7
  0.6 0.8 %constant_dynamic-update-slice_fusion.1 = bf16[64,512]{1,0:T(8,128)(2,1)S(1)} fusion(bf16[64,256]{1,0:T(8,128)(2,1)} %param.12), kind=kLoop, calls=%fused_computation.3 | loop fusion | bytes 65536
  1.4 0.0 copy-done.7
  1.4 4.1 %collective-permute-start = (bf16[64,512]{1,0:T(8,128)(2,1)S(1)}, bf16[64,512]{1,0:T(8,128)(2,1)S(1)}, u32[]{:S(2)}, u32[]{:S(2)}) collective-permute-start(bf16[64,512]{1,0:T(8,128)(2,1)S(1)} %constant_dynamic-update-slice_fusion), channel_id=1, source_target_pairs={{0,8},{2,10},{4,12},{6,14},{8,0},{10,2},{12,4},{14,6},{1,9},{3,11}... | collective-permute-start | bytes 196616 | tf_op jit(solution)/shard_map/ppermute | solution.py:328
  5.5 3.6 %collective-permute-done = bf16[64,512]{1,0:T(8,128)(2,1)S(1)} collective-permute-done((bf16[64,512]{1,0:T(8,128)(2,1)S(1)}, bf16[64,512]{1,0:T(8,128)(2,1)S(1)}, u32[]{:S(2)}, u32[]{:S(2)}) %collective-permute-start) | collective-permute-done | bytes 65568 | tf_op jit(solution)/shard_map/ppermute | solution.py:328
  9.2 0.0 copy-start.1
  9.2 0.0 copy-start.2
  9.2 0.0 copy-start.3
  9.2 0.6 %collective-permute-start.1 = (bf16[128,512]{1,0:T(8,128)(2,1)S(1)}, bf16[128,512]{1,0:T(8,128)(2,1)S(1)}, u32[]{:S(2)}, u32[]{:S(2)}) collective-permute-start(bf16[128,512]{1,0:T(8,128)(2,1)S(1)} %pad_maximum_fusion.1), channel_id=1, source_target_pairs={{0,4},{2,6},{4,0},{6,2},{8,12},{10,14},{12,8},{14,10},{1,5},{3,7},... | collective-permute-start | bytes 393224 | tf_op jit(solution)/shard_map/ppermute | solution.py:328
  9.9 4.4 %collective-permute-done.1 = bf16[128,512]{1,0:T(8,128)(2,1)S(1)} collective-permute-done((bf16[128,512]{1,0:T(8,128)(2,1)S(1)}, bf16[128,512]{1,0:T(8,128)(2,1)S(1)}, u32[]{:S(2)}, u32[]{:S(2)}) %collective-permute-start.1) | collective-permute-done | bytes 131104 | tf_op jit(solution)/shard_map/ppermute | solution.py:328
  14.3 0.1 collective-permute-start.4
  14.4 1.8 %collective-permute-start.2 = (bf16[256,512]{1,0:T(8,128)(2,1)S(1)}, bf16[256,512]{1,0:T(8,128)(2,1)S(1)}, u32[]{:S(2)}, u32[]{:S(2)}) collective-permute-start(bf16[256,512]{1,0:T(8,128)(2,1)S(1)} %pad_maximum_fusion.refs_0_), channel_id=1, source_target_pairs={{0,2},{2,0},{4,6},{6,4},{8,10},{10,8},{12,14},{14,12},{1,3},{3,1},... | collective-permute-start | bytes 786440 | tf_op jit(solution)/shard_map/ppermute | solution.py:328
  16.1 0.0 copy-done.1
  16.1 0.0 copy-done.2
  16.1 0.0 copy-done.3
  16.2 3.4 %decode_local.1.a_ref = bf16[10,16,128]{2,1,0:T(8,128)(2,1)S(1)} custom-call(s32[16]{0:T(128)} %lens.1, bf16[16,896]{1,0:T(8,128)(2,1)S(1)} %copy-done.1, bf16[16,128]{1,0:T(8,128)(2,1)S(1)} %copy-done.2, bf16[16,128]{1,0:T(8,128)(2,1)S(1)} %copy-done.3, bf16[16,1,256,128]{3,2,1,0:T(8,128)(2,1)} %k_ref.1, bf16[16,1,256,128]{3,2,1,0:T(8,128)(2,1)} %v_ref.1), custom_call_target="tpu_custom_call" | custom-call | flops 2000000000 | bytes 2097152 | tf_op jit(solution)/shard_map/decode_local/pallas_call | solution.py:131
  19.6 0.0 copy-start
  19.6 0.4 %collective-permute-start.5 = (bf16[10,16,128]{2,1,0:T(8,128)(2,1)S(1)}, bf16[10,16,128]{2,1,0:T(8,128)(2,1)S(1)}, u32[]{:S(2)}, u32[]{:S(2)}) collective-permute-start(bf16[10,16,128]{2,1,0:T(8,128)(2,1)S(1)} %decode_local.1.a_ref), channel_id=1, source_target_pairs={{0,4},{2,6},{4,0},{6,2},{8,12},{10,14},{12,8},{14,10},{1,5},{3,7},... | collective-permute-start | bytes 122888 | tf_op jit(solution)/shard_map/ppermute | solution.py:328
  20.0 3.6 %collective-permute-done.5.b_ref = bf16[10,16,128]{2,1,0:T(8,128)(2,1)S(1)} collective-permute-done((bf16[10,16,128]{2,1,0:T(8,128)(2,1)S(1)}, bf16[10,16,128]{2,1,0:T(8,128)(2,1)S(1)}, u32[]{:S(2)}, u32[]{:S(2)}) %collective-permute-start.5) | collective-permute-done | bytes 40992 | tf_op jit(solution)/shard_map/ppermute | solution.py:328
  23.7 0.1 decode_merge.3.a_ref
  23.8 0.4 collective-permute-start.6
  24.2 3.7 %collective-permute-done.6.b_ref = bf16[10,16,128]{2,1,0:T(8,128)(2,1)S(1)} collective-permute-done((bf16[10,16,128]{2,1,0:T(8,128)(2,1)S(1)}, bf16[10,16,128]{2,1,0:T(8,128)(2,1)S(1)}, u32[]{:S(2)}, u32[]{:S(2)}) %collective-permute-start.6) | collective-permute-done | bytes 40992 | tf_op jit(solution)/shard_map/ppermute | solution.py:328
  27.8 0.1 decode_merge.4.a_ref
  28.0 2.2 %collective-permute-start.7 = (bf16[10,16,128]{2,1,0:T(8,128)(2,1)S(1)}, bf16[10,16,128]{2,1,0:T(8,128)(2,1)S(1)}, u32[]{:S(2)}, u32[]{:S(2)}) collective-permute-start(bf16[10,16,128]{2,1,0:T(8,128)(2,1)S(1)} %decode_merge.4.a_ref), channel_id=1, source_target_pairs={{0,8},{2,10},{4,12},{6,14},{8,0},{10,2},{12,4},{14,6},{1,9},{3,11}... | collective-permute-start | bytes 122888 | tf_op jit(solution)/shard_map/ppermute | solution.py:328
  30.8 2.1 %collective-permute-done.7.b_ref = bf16[10,16,128]{2,1,0:T(8,128)(2,1)S(1)} collective-permute-done((bf16[10,16,128]{2,1,0:T(8,128)(2,1)S(1)}, bf16[10,16,128]{2,1,0:T(8,128)(2,1)S(1)}, u32[]{:S(2)}, u32[]{:S(2)}) %collective-permute-start.7) | collective-permute-done | bytes 40992 | tf_op jit(solution)/shard_map/ppermute | solution.py:328
  33.0 0.7 %decode_merge.5 = bf16[16,896]{1,0:T(8,128)(2,1)} custom-call(bf16[10,16,128]{2,1,0:T(8,128)(2,1)S(1)} %decode_merge.4.a_ref, bf16[10,16,128]{2,1,0:T(8,128)(2,1)S(1)} %collective-permute-done.7.b_ref), custom_call_target="tpu_custom_call" | custom-call | tf_op jit(solution)/shard_map/decode_merge/pallas_call | solution.py:172
  33.7 0.0 collective-permute-done.2.refs_0_
  33.7 0.0 collective-permute-start.3
  33.7 0.0 collective-permute-done.4.refs_1_
  33.7 0.0 copy-done
  33.7 1.8 %attend.2 = (f32[2,448,128]{2,1,0:T(8,128)S(1)}, f32[2,448,128]{2,1,0:T(8,128)S(1)}, f32[2,448,128]{2,1,0:T(8,128)S(1)}) custom-call(s32[16]{0:T(128)} %span_ref.3, s32[1]{0:T(128)S(6)} %copy.14.len_ref, bf16[64,1792]{1,0:T(8,128)(2,1)S(1)} %copy-done, bf16[256,512]{1,0:T(8,128)(2,1)S(1)} %pad_maximum_fusion.refs_0_, ...), custom_call_target="tpu_custom_call" | custom-call | flops 4000000000 | bytes 229376 | tf_op jit(solution)/shard_map/attend/pallas_call | solution.py:297
  35.5 0.0 copy-start.4
  35.5 0.8 %copy-done.4 = f32[2,448,128]{2,1,0:T(8,128)} copy-done((f32[2,448,128]{2,1,0:T(8,128)}, f32[2,448,128]{2,1,0:T(8,128)S(1)}, u32[]{:S(2)}) %copy-start.4) | copy-done | bytes 458776
  36.3 0.0 copy-start.5
  36.3 0.8 %copy-done.5 = f32[2,448,128]{2,1,0:T(8,128)} copy-done((f32[2,448,128]{2,1,0:T(8,128)}, f32[2,448,128]{2,1,0:T(8,128)S(1)}, u32[]{:S(2)}) %copy-start.5) | copy-done | bytes 458776
  37.0 0.0 copy-start.6
  37.0 0.8 %copy-done.6 = f32[2,448,128]{2,1,0:T(8,128)} copy-done((f32[2,448,128]{2,1,0:T(8,128)}, f32[2,448,128]{2,1,0:T(8,128)S(1)}, u32[]{:S(2)}) %copy-start.6) | copy-done | bytes 458776
  37.8 0.0 collective-permute-done.3.refs_1_
  37.8 4.7 %attend.3 = bf16[64,1792]{1,0:T(8,128)(2,1)} custom-call(s32[16]{0:T(128)} %span_ref.3, s32[1]{0:T(128)S(6)} %copy.14.len_ref, bf16[64,1792]{1,0:T(8,128)(2,1)S(1)} %copy-done, bf16[256,512]{1,0:T(8,128)(2,1)S(1)} %collective-permute-done.2.refs_0_, bf16[256,512]{1,0:T(8,128)(2,1)S(1)} %collective-permute-done.3.refs_1_, f32[2,448,128]{2,1,0:T(8,128)} %copy-done.4, ...), custom_call_target="tpu_custom_call" | custom-call | flops 4000000000 | bytes 229376 | tf_op jit(solution)/shard_map/attend/pallas_call | solution.py:297
  (3 shorter events, 0.0 us)
Async XLA Ops:
  0.6 0.8 %copy-start.7 = (bf16[64,256]{1,0:T(8,128)(2,1)S(1)}, bf16[64,256]{1,0:T(8,128)(2,1)}, u32[]{:S(2)}) copy-start(bf16[64,256]{1,0:T(8,128)(2,1)} %param.13) | copy-start | bytes 98308
  1.4 7.8 %collective-permute-start = (bf16[64,512]{1,0:T(8,128)(2,1)S(1)}, bf16[64,512]{1,0:T(8,128)(2,1)S(1)}, u32[]{:S(2)}, u32[]{:S(2)}) collective-permute-start(bf16[64,512]{1,0:T(8,128)(2,1)S(1)} %constant_dynamic-update-slice_fusion), channel_id=1, source_target_pairs={{0,8},{2,10},{4,12},{6,14},{8,0},{10,2},{12,4},{14,6},{1,9},{3,11}... | collective-permute-start | bytes 196616 | tf_op jit(solution)/shard_map/ppermute | solution.py:328
  9.2 6.9 %copy-start.1 = (bf16[16,896]{1,0:T(8,128)(2,1)S(1)}, bf16[16,896]{1,0:T(8,128)(2,1)}, u32[]{:S(2)}) copy-start(bf16[16,896]{1,0:T(8,128)(2,1)} %q_ref.5) | copy-start | bytes 86020
  9.2 6.9 %copy-start.2 = (bf16[16,128]{1,0:T(8,128)(2,1)S(1)}, bf16[16,128]{1,0:T(8,128)(2,1)}, u32[]{:S(2)}) copy-start(bf16[16,128]{1,0:T(8,128)(2,1)} %nk_ref.1) | copy-start | bytes 12292
  9.2 6.9 %copy-start.3 = (bf16[16,128]{1,0:T(8,128)(2,1)S(1)}, bf16[16,128]{1,0:T(8,128)(2,1)}, u32[]{:S(2)}) copy-start(bf16[16,128]{1,0:T(8,128)(2,1)} %nv_ref.1) | copy-start | bytes 12292
  9.2 5.0 %collective-permute-start.1 = (bf16[128,512]{1,0:T(8,128)(2,1)S(1)}, bf16[128,512]{1,0:T(8,128)(2,1)S(1)}, u32[]{:S(2)}, u32[]{:S(2)}) collective-permute-start(bf16[128,512]{1,0:T(8,128)(2,1)S(1)} %pad_maximum_fusion.1), channel_id=1, source_target_pairs={{0,4},{2,6},{4,0},{6,2},{8,12},{10,14},{12,8},{14,10},{1,5},{3,7},... | collective-permute-start | bytes 393224 | tf_op jit(solution)/shard_map/ppermute | solution.py:328
  14.3 19.4 %collective-permute-start.4 = (bf16[256,512]{1,0:T(8,128)(2,1)S(1)}, bf16[256,512]{1,0:T(8,128)(2,1)S(1)}, u32[]{:S(2)}, u32[]{:S(2)}) collective-permute-start(bf16[256,512]{1,0:T(8,128)(2,1)S(1)} %pad_maximum_fusion.refs_0_), channel_id=1, source_target_pairs={{0,1},{1,0},{2,3},{3,2},{4,5},{5,4},{6,7},{7,6},{8,9},{9,8},{10,11... | collective-permute-start | bytes 786440 | tf_op jit(solution)/shard_map/ppermute | solution.py:331
  14.4 19.3 %collective-permute-start.2 = (bf16[256,512]{1,0:T(8,128)(2,1)S(1)}, bf16[256,512]{1,0:T(8,128)(2,1)S(1)}, u32[]{:S(2)}, u32[]{:S(2)}) collective-permute-start(bf16[256,512]{1,0:T(8,128)(2,1)S(1)} %pad_maximum_fusion.refs_0_), channel_id=1, source_target_pairs={{0,2},{2,0},{4,6},{6,4},{8,10},{10,8},{12,14},{14,12},{1,3},{3,1},... | collective-permute-start | bytes 786440 | tf_op jit(solution)/shard_map/ppermute | solution.py:328
  19.6 14.1 %copy-start = (bf16[64,1792]{1,0:T(8,128)(2,1)S(1)}, bf16[64,1792]{1,0:T(8,128)(2,1)}, u32[]{:S(2)}) copy-start(bf16[64,1792]{1,0:T(8,128)(2,1)} %q_ref.4) | copy-start | bytes 688132
  19.6 4.1 %collective-permute-start.5 = (bf16[10,16,128]{2,1,0:T(8,128)(2,1)S(1)}, bf16[10,16,128]{2,1,0:T(8,128)(2,1)S(1)}, u32[]{:S(2)}, u32[]{:S(2)}) collective-permute-start(bf16[10,16,128]{2,1,0:T(8,128)(2,1)S(1)} %decode_local.1.a_ref), channel_id=1, source_target_pairs={{0,4},{2,6},{4,0},{6,2},{8,12},{10,14},{12,8},{14,10},{1,5},{3,7},... | collective-permute-start | bytes 122888 | tf_op jit(solution)/shard_map/ppermute | solution.py:328
  23.8 4.1 %collective-permute-start.6 = (bf16[10,16,128]{2,1,0:T(8,128)(2,1)S(1)}, bf16[10,16,128]{2,1,0:T(8,128)(2,1)S(1)}, u32[]{:S(2)}, u32[]{:S(2)}) collective-permute-start(bf16[10,16,128]{2,1,0:T(8,128)(2,1)S(1)} %decode_merge.3.a_ref), channel_id=1, source_target_pairs={{0,2},{2,0},{4,6},{6,4},{8,10},{10,8},{12,14},{14,12},{1,3},{3,1},... | collective-permute-start | bytes 122888 | tf_op jit(solution)/shard_map/ppermute | solution.py:328
  28.0 5.0 %collective-permute-start.7 = (bf16[10,16,128]{2,1,0:T(8,128)(2,1)S(1)}, bf16[10,16,128]{2,1,0:T(8,128)(2,1)S(1)}, u32[]{:S(2)}, u32[]{:S(2)}) collective-permute-start(bf16[10,16,128]{2,1,0:T(8,128)(2,1)S(1)} %decode_merge.4.a_ref), channel_id=1, source_target_pairs={{0,8},{2,10},{4,12},{6,14},{8,0},{10,2},{12,4},{14,6},{1,9},{3,11}... | collective-permute-start | bytes 122888 | tf_op jit(solution)/shard_map/ppermute | solution.py:328
  33.7 4.1 %collective-permute-start.3 = (bf16[256,512]{1,0:T(8,128)(2,1)S(1)}, bf16[256,512]{1,0:T(8,128)(2,1)S(1)}, u32[]{:S(2)}, u32[]{:S(2)}) collective-permute-start(bf16[256,512]{1,0:T(8,128)(2,1)S(1)} %collective-permute-done.2.refs_0_), channel_id=1, source_target_pairs={{0,1},{1,0},{2,3},{3,2},{4,5},{5,4},{6,7},{7,6},{8,9},{9,8},{10,11... | collective-permute-start | bytes 786440 | tf_op jit(solution)/shard_map/ppermute | solution.py:331
  35.5 0.8 %copy-start.4 = (f32[2,448,128]{2,1,0:T(8,128)}, f32[2,448,128]{2,1,0:T(8,128)S(1)}, u32[]{:S(2)}) copy-start(f32[2,448,128]{2,1,0:T(8,128)S(1)} %get-tuple-element.5.refs_2_) | copy-start | bytes 1376260
  36.3 0.8 %copy-start.5 = (f32[2,448,128]{2,1,0:T(8,128)}, f32[2,448,128]{2,1,0:T(8,128)S(1)}, u32[]{:S(2)}) copy-start(f32[2,448,128]{2,1,0:T(8,128)S(1)} %get-tuple-element.6.refs_3_) | copy-start | bytes 1376260
  37.0 0.8 %copy-start.6 = (f32[2,448,128]{2,1,0:T(8,128)}, f32[2,448,128]{2,1,0:T(8,128)S(1)}, u32[]{:S(2)}) copy-start(f32[2,448,128]{2,1,0:T(8,128)S(1)} %get-tuple-element.7.refs_4_) | copy-start | bytes 1376260
where the time goes:
time: 42.8 us; the launch traced here: 42.6 us
  waiting for transfers between devices  17.5 us (41%)
  Pallas kernels  10.9 us (25%)
  starting transfers between devices  9.6 us (22%)
  local copies, waits for them, and re-layouts  3.12 us (7%)
  between operations  1.39 us (3%)
    ppermute x6, waiting for transfers between devices, swap(): return lax.ppermute(x, 'seq', [(i, i ^ bit) for i in range(seq)])  17.5 us
    ppermute x6, starting transfers between devices, swap(): return lax.ppermute(x, 'seq', [(i, i ^ bit) for i in range(seq)])  9.53 us
    pallas_call x2, Pallas kernels, attend(): pl.pallas_call(functools.partial(attend_kernel, bases=bases, bits=bits, f...  6.51 us
    pallas_call x1, Pallas kernels, decode_local(): pl.pallas_call(decode_kernel, grid=(sessions // per_step,), in_specs=[in_...  3.41 us
    unnamed x17, local copies, waits for them, and re-layouts  3.12 us
    pallas_call x3, Pallas kernels, merge(): pl.pallas_call(functools.partial(merge_kernel, final=final), in_specs=[in...  0.99 us
  transfers between devices with their start and end apart: 8, of which 5 were waited for; matrix products, arithmetic and copies ran while one was open for 0% of the time, Pallas kernels for 15%

commit v1 on v0

--- a/solution.py
+++ b/solution.py
@@ -139,6 +139,7 @@
         cost_estimate=pl.CostEstimate(
             flops=2_000_000_000, bytes_accessed=cache_key.size * 4, transcendentals=0
         ),
+        compiler_params=pltpu.CompilerParams(vmem_limit_bytes=16 << 20),
         name="decode_local",
     )(lens, vmem(query), vmem(new_key), vmem(new_value), cache_key, cache_value)
 
@@ -176,6 +177,7 @@
         out_shape=jax.ShapeDtypeStruct(shape, jnp.bfloat16)
         if final
         else pltpu.VMEM(shape, jnp.bfloat16),
+        compiler_params=pltpu.CompilerParams(vmem_limit_bytes=8 << 20),
         name="decode_merge",
     )(vmem(a), vmem(b))
 
@@ -183,7 +185,7 @@
 def attend_kernel(span_ref, len_ref, q_ref, *refs, bases, bits, first, last):
     kv_refs, refs = refs[: len(bases)], refs[len(bases) :]
     if not first:
-        state_in, refs = refs[:3], refs[3:]
+        state_in, refs = refs[0], refs[1:]
     rows = q_ref.shape[0]
     group = QH // KVH
     scale = math.log2(math.e) / math.sqrt(HD)
@@ -206,7 +208,9 @@
                 )
             )
         else:
-            state.append((state_in[0][g], state_in[1][g][:, :1], state_in[2][g][:, :1]))
+            state.append(
+                (state_in[g, :, :HD], state_in[g, :, HD : HD + 1], state_in[g, :, 2 * HD - 1 :])
+            )
     queries = [
         jnp.concatenate(
             [q_ref[:, (g * group + h) * HD : (g * group + h + 1) * HD] for h in range(group)], axis=0
@@ -284,28 +288,31 @@
                 part = out[h * rows : (h + 1) * rows]
                 refs[0][:, at : at + HD] = jnp.where(live, part, 0.0).astype(jnp.bfloat16)
     else:
+        lane = lax.broadcasted_iota(jnp.int32, (group * rows, HD), 1)
         for g in range(KVH):
-            for ref, value in zip(refs, state[g]):
-                ref[g] = jnp.broadcast_to(value, ref.shape[1:])
+            acc, top, total = state[g]
+            refs[0][g, :, :HD] = acc
+            refs[0][g, :, HD:] = jnp.where(lane < HD // 2, top, total)
 
 
 def attend(spans, length, query, pieces, bases, bits, state, last):
     rows = query.shape[0]
     first = state is None
-    shape = (KVH, QH // KVH * rows, HD)
-    operands = [query, *pieces] + ([] if first else list(state))
+    shape = (KVH, QH // KVH * rows, 2 * HD)
+    operands = [query, *pieces] + ([] if first else [state])
     return pl.pallas_call(
         functools.partial(attend_kernel, bases=bases, bits=bits, first=first, last=last),
         in_specs=[in_smem(), in_smem()] + [in_vmem()] * len(operands),
-        out_specs=in_vmem() if last else [in_vmem()] * 3,
+        out_specs=in_vmem(),
         out_shape=jax.ShapeDtypeStruct(query.shape, jnp.bfloat16)
         if last
-        else [pltpu.VMEM(shape, jnp.float32)] * 3,
+        else pltpu.VMEM(shape, jnp.float32),
         cost_estimate=pl.CostEstimate(
             flops=4_000_000_000, bytes_accessed=query.size * 2, transcendentals=0
         ),
+        compiler_params=pltpu.CompilerParams(vmem_limit_bytes=32 << 20),
         name="attend",
-    )(spans, length, *(vmem(x) for x in operands[: 1 + len(pieces)]), *operands[1 + len(pieces) :])
+    )(spans, length, *(vmem(x) for x in operands))
 
 
 def per_device(

time: 42.8 us -> 41.1 us (0.960)
  Pallas kernels: 10.9 us -> 9.03 us
    pallas_call x1, Pallas kernels: 3.41 us -> 2.23 us  [decode_local(): pl.pallas_call(decode_kernel, grid=(sessions // per_step,), in_specs=[in_...]
    pallas_call x2, Pallas kernels: 6.51 us -> 5.81 us  [attend(): pl.pallas_call(functools.partial(attend_kernel, bases=bases, bits=bits, f...]
    unnamed x17 -> x19, local copies, waits for them, and re-layouts: 3.12 us -> 3.25 us
  transfers between devices with their start and end apart: 8 -> 8, of which waited for: 5 -> 5; matrix products, arithmetic and copies ran while one was open for 0% -> 0% of each run, Pallas kernels for 15% -> 12%
where the time goes in v1:
time: 41.1 us; the launch traced here: 40.8 us
  waiting for transfers between devices  17.5 us (43%)
  starting transfers between devices  9.6 us (23%)
  Pallas kernels  9.03 us (22%)
  local copies, waits for them, and re-layouts  3.26 us (8%)
  between operations  1.43 us (3%)
    ppermute x6, waiting for transfers between devices, swap(): return lax.ppermute(x, 'seq', [(i, i ^ bit) for i in range(seq)])  17.5 us
    ppermute x6, starting transfers between devices, swap(): return lax.ppermute(x, 'seq', [(i, i ^ bit) for i in range(seq)])  9.53 us
    pallas_call x2, Pallas kernels, attend(): pl.pallas_call(functools.partial(attend_kernel, bases=bases, bits=bits, f...  5.81 us
    unnamed x19, local copies, waits for them, and re-layouts  3.25 us
    pallas_call x1, Pallas kernels, decode_local(): pl.pallas_call(decode_kernel, grid=(sessions // per_step,), in_specs=[in_...  2.23 us
    pallas_call x3, Pallas kernels, merge(): pl.pallas_call(functools.partial(merge_kernel, final=final), in_specs=[in...  0.99 us
  transfers between devices with their start and end apart: 8, of which 5 were waited for; matrix products, arithmetic and copies ran while one was open for 0% of the time, Pallas kernels for 12%

profile of v1, /device:TPU:0, one launch (start us, length us, event | category | flops | bytes accessed | tf_op | source)
XLA Modules:
  0.0 40.8 jit_solution(16005807974073418443)
XLA Ops:
  0.6 0.0 copy-start.8
  0.6 0.8 %constant_dynamic-update-slice_fusion.1 = bf16[64,512]{1,0:T(8,128)(2,1)S(1)} fusion(bf16[64,256]{1,0:T(8,128)(2,1)} %param.12), kind=kLoop, calls=%fused_computation.3 | loop fusion | bytes 65536
  1.4 0.0 copy-done.8
  1.4 4.1 %collective-permute-start = (bf16[64,512]{1,0:T(8,128)(2,1)S(1)}, bf16[64,512]{1,0:T(8,128)(2,1)S(1)}, u32[]{:S(2)}, u32[]{:S(2)}) collective-permute-start(bf16[64,512]{1,0:T(8,128)(2,1)S(1)} %constant_dynamic-update-slice_fusion), channel_id=1, source_target_pairs={{0,8},{2,10},{4,12},{6,14},{8,0},{10,2},{12,4},{14,6},{1,9},{3,11}... | collective-permute-start | bytes 196616 | tf_op jit(solution)/shard_map/ppermute | solution.py:335
  5.5 3.6 %collective-permute-done = bf16[64,512]{1,0:T(8,128)(2,1)S(1)} collective-permute-done((bf16[64,512]{1,0:T(8,128)(2,1)S(1)}, bf16[64,512]{1,0:T(8,128)(2,1)S(1)}, u32[]{:S(2)}, u32[]{:S(2)}) %collective-permute-start) | collective-permute-done | bytes 65568 | tf_op jit(solution)/shard_map/ppermute | solution.py:335
  9.2 0.0 copy-start.3
  9.2 0.0 copy-start.4
  9.2 0.0 copy-start.5
  9.2 0.0 copy-start.6
  9.3 0.6 %collective-permute-start.1 = (bf16[128,512]{1,0:T(8,128)(2,1)S(1)}, bf16[128,512]{1,0:T(8,128)(2,1)S(1)}, u32[]{:S(2)}, u32[]{:S(2)}) collective-permute-start(bf16[128,512]{1,0:T(8,128)(2,1)S(1)} %pad_maximum_fusion.1), channel_id=1, source_target_pairs={{0,4},{2,6},{4,0},{6,2},{8,12},{10,14},{12,8},{14,10},{1,5},{3,7},... | collective-permute-start | bytes 393224 | tf_op jit(solution)/shard_map/ppermute | solution.py:335
  9.9 4.4 %collective-permute-done.1 = bf16[128,512]{1,0:T(8,128)(2,1)S(1)} collective-permute-done((bf16[128,512]{1,0:T(8,128)(2,1)S(1)}, bf16[128,512]{1,0:T(8,128)(2,1)S(1)}, u32[]{:S(2)}, u32[]{:S(2)}) %collective-permute-start.1) | collective-permute-done | bytes 131104 | tf_op jit(solution)/shard_map/ppermute | solution.py:335
  14.3 0.1 collective-permute-start.4
  14.4 1.8 %collective-permute-start.2 = (bf16[256,512]{1,0:T(8,128)(2,1)S(1)}, bf16[256,512]{1,0:T(8,128)(2,1)S(1)}, u32[]{:S(2)}, u32[]{:S(2)}) collective-permute-start(bf16[256,512]{1,0:T(8,128)(2,1)S(1)} %pad_maximum_fusion.refs_0_), channel_id=1, source_target_pairs={{0,2},{2,0},{4,6},{6,4},{8,10},{10,8},{12,14},{14,12},{1,3},{3,1},... | collective-permute-start | bytes 786440 | tf_op jit(solution)/shard_map/ppermute | solution.py:335
  16.2 0.0 copy-done.3
  16.2 0.0 copy-done.4
  16.2 0.0 copy-done.5
  16.2 0.0 copy-done.6
  16.2 0.0 copy-start
  16.2 1.2 %copy-done = bf16[16,1,256,128]{3,2,1,0:T(8,128)(2,1)S(1)} copy-done((bf16[16,1,256,128]{3,2,1,0:T(8,128)(2,1)S(1)}, bf16[16,1,256,128]{3,2,1,0:T(8,128)(2,1)}, u32[]{:S(2)}) %copy-start) | copy-done | bytes 1048600
  17.4 0.0 copy-start.1
  17.4 1.2 %copy-done.1 = bf16[16,1,256,128]{3,2,1,0:T(8,128)(2,1)S(1)} copy-done((bf16[16,1,256,128]{3,2,1,0:T(8,128)(2,1)S(1)}, bf16[16,1,256,128]{3,2,1,0:T(8,128)(2,1)}, u32[]{:S(2)}) %copy-start.1) | copy-done | bytes 1048600
  18.6 2.2 %decode_local.1.a_ref = bf16[10,16,128]{2,1,0:T(8,128)(2,1)S(1)} custom-call(s32[16]{0:T(128)S(1)} %copy-done.6, bf16[16,896]{1,0:T(8,128)(2,1)S(1)} %copy-done.3, bf16[16,128]{1,0:T(8,128)(2,1)S(1)} %copy-done.4, bf16[16,128]{1,0:T(8,128)(2,1)S(1)} %copy-done.5, bf16[16,1,256,128]{3,2,1,0:T(8,128)(2,1)S(1)} %copy-done, bf16[16,1,256,128]{3,2,1,0:T(8,128)(2,1)S(1)} %copy-done.1), custom_call_target="tpu_custom_call" | custom-call | flops 2000000000 | bytes 2097152 | tf_op jit(solution)/shard_map/decode_local/pallas_call | solution.py:131
  20.9 0.0 copy-start.2
  20.9 0.4 %collective-permute-start.5 = (bf16[10,16,128]{2,1,0:T(8,128)(2,1)S(1)}, bf16[10,16,128]{2,1,0:T(8,128)(2,1)S(1)}, u32[]{:S(2)}, u32[]{:S(2)}) collective-permute-start(bf16[10,16,128]{2,1,0:T(8,128)(2,1)S(1)} %decode_local.1.a_ref), channel_id=1, source_target_pairs={{0,4},{2,6},{4,0},{6,2},{8,12},{10,14},{12,8},{14,10},{1,5},{3,7},... | collective-permute-start | bytes 122888 | tf_op jit(solution)/shard_map/ppermute | solution.py:335
  21.3 3.6 %collective-permute-done.5.b_ref = bf16[10,16,128]{2,1,0:T(8,128)(2,1)S(1)} collective-permute-done((bf16[10,16,128]{2,1,0:T(8,128)(2,1)S(1)}, bf16[10,16,128]{2,1,0:T(8,128)(2,1)S(1)}, u32[]{:S(2)}, u32[]{:S(2)}) %collective-permute-start.5) | collective-permute-done | bytes 40992 | tf_op jit(solution)/shard_map/ppermute | solution.py:335
  24.9 0.1 decode_merge.3.a_ref
  25.1 0.4 collective-permute-start.6
  25.5 3.7 %collective-permute-done.6.b_ref = bf16[10,16,128]{2,1,0:T(8,128)(2,1)S(1)} collective-permute-done((bf16[10,16,128]{2,1,0:T(8,128)(2,1)S(1)}, bf16[10,16,128]{2,1,0:T(8,128)(2,1)S(1)}, u32[]{:S(2)}, u32[]{:S(2)}) %collective-permute-start.6) | collective-permute-done | bytes 40992 | tf_op jit(solution)/shard_map/ppermute | solution.py:335
  29.1 0.1 decode_merge.4.a_ref
  29.3 2.2 %collective-permute-start.7 = (bf16[10,16,128]{2,1,0:T(8,128)(2,1)S(1)}, bf16[10,16,128]{2,1,0:T(8,128)(2,1)S(1)}, u32[]{:S(2)}, u32[]{:S(2)}) collective-permute-start(bf16[10,16,128]{2,1,0:T(8,128)(2,1)S(1)} %decode_merge.4.a_ref), channel_id=1, source_target_pairs={{0,8},{2,10},{4,12},{6,14},{8,0},{10,2},{12,4},{14,6},{1,9},{3,11}... | collective-permute-start | bytes 122888 | tf_op jit(solution)/shard_map/ppermute | solution.py:335
  32.1 0.0 copy-start.7
  32.1 2.1 %collective-permute-done.7.b_ref = bf16[10,16,128]{2,1,0:T(8,128)(2,1)S(1)} collective-permute-done((bf16[10,16,128]{2,1,0:T(8,128)(2,1)S(1)}, bf16[10,16,128]{2,1,0:T(8,128)(2,1)S(1)}, u32[]{:S(2)}, u32[]{:S(2)}) %collective-permute-start.7) | collective-permute-done | bytes 40992 | tf_op jit(solution)/shard_map/ppermute | solution.py:335
  34.2 0.7 %decode_merge.5 = bf16[16,896]{1,0:T(8,128)(2,1)} custom-call(bf16[10,16,128]{2,1,0:T(8,128)(2,1)S(1)} %decode_merge.4.a_ref, bf16[10,16,128]{2,1,0:T(8,128)(2,1)S(1)} %collective-permute-done.7.b_ref), custom_call_target="tpu_custom_call" | custom-call | tf_op jit(solution)/shard_map/decode_merge/pallas_call | solution.py:173
  35.0 0.0 collective-permute-done.2.refs_0_
  35.0 0.0 collective-permute-start.3
  35.0 0.0 collective-permute-done.4.refs_1_
  35.0 0.0 copy-done.2
  35.0 0.0 copy-done.7
  35.0 1.7 %attend.2.refs_2_ = f32[2,448,256]{2,1,0:T(8,128)S(1)} custom-call(s32[16]{0:T(128)S(1)} %copy-done.7, s32[1]{0:T(128)S(6)} %copy.14.len_ref, bf16[64,1792]{1,0:T(8,128)(2,1)S(1)} %copy-done.2, bf16[256,512]{1,0:T(8,128)(2,1)S(1)} %pad_maximum_fusion.refs_0_, bf16[256,512]{1,0:T(8,128)(2,1)S(1)} %collective-permute-done.4.refs_1_), custom_call_target="tpu_custom_call" | custom-call | flops 4000000000 | bytes 229376 | tf_op jit(solution)/shard_map/attend/pallas_call | solution.py:303
  36.7 0.0 collective-permute-done.3.refs_1_
  36.7 4.1 %attend.3 = bf16[64,1792]{1,0:T(8,128)(2,1)} custom-call(s32[16]{0:T(128)S(1)} %copy-done.7, s32[1]{0:T(128)S(6)} %copy.14.len_ref, bf16[64,1792]{1,0:T(8,128)(2,1)S(1)} %copy-done.2, bf16[256,512]{1,0:T(8,128)(2,1)S(1)} %collective-permute-done.2.refs_0_, bf16[256,512]{1,0:T(8,128)(2,1)S(1)} %collective-permute-done.3.refs_1_, f32[2,448,256]{2,1,0:T(8,128)S(1)} %attend.2.refs_2_), custom_call_target="tpu_custom_call" | custom-call | flops 4000000000 | bytes 229376 | tf_op jit(solution)/shard_map/attend/pallas_call | solution.py:303
  (3 shorter events, 0.0 us)
Async XLA Ops:
  0.6 0.8 %copy-start.8 = (bf16[64,256]{1,0:T(8,128)(2,1)S(1)}, bf16[64,256]{1,0:T(8,128)(2,1)}, u32[]{:S(2)}) copy-start(bf16[64,256]{1,0:T(8,128)(2,1)} %param.13) | copy-start | bytes 98308
  1.4 7.8 %collective-permute-start = (bf16[64,512]{1,0:T(8,128)(2,1)S(1)}, bf16[64,512]{1,0:T(8,128)(2,1)S(1)}, u32[]{:S(2)}, u32[]{:S(2)}) collective-permute-start(bf16[64,512]{1,0:T(8,128)(2,1)S(1)} %constant_dynamic-update-slice_fusion), channel_id=1, source_target_pairs={{0,8},{2,10},{4,12},{6,14},{8,0},{10,2},{12,4},{14,6},{1,9},{3,11}... | collective-permute-start | bytes 196616 | tf_op jit(solution)/shard_map/ppermute | solution.py:335
  9.2 6.9 %copy-start.3 = (bf16[16,896]{1,0:T(8,128)(2,1)S(1)}, bf16[16,896]{1,0:T(8,128)(2,1)}, u32[]{:S(2)}) copy-start(bf16[16,896]{1,0:T(8,128)(2,1)} %q_ref.5) | copy-start | bytes 86020
  9.2 6.9 %copy-start.4 = (bf16[16,128]{1,0:T(8,128)(2,1)S(1)}, bf16[16,128]{1,0:T(8,128)(2,1)}, u32[]{:S(2)}) copy-start(bf16[16,128]{1,0:T(8,128)(2,1)} %nk_ref.1) | copy-start | bytes 12292
  9.2 6.9 %copy-start.5 = (bf16[16,128]{1,0:T(8,128)(2,1)S(1)}, bf16[16,128]{1,0:T(8,128)(2,1)}, u32[]{:S(2)}) copy-start(bf16[16,128]{1,0:T(8,128)(2,1)} %nv_ref.1) | copy-start | bytes 12292
  9.2 6.9 %copy-start.6 = (s32[16]{0:T(128)S(1)}, s32[16]{0:T(128)}, u32[]{:S(2)}) copy-start(s32[16]{0:T(128)} %lens.1) | copy-start | bytes 196
  9.3 5.0 %collective-permute-start.1 = (bf16[128,512]{1,0:T(8,128)(2,1)S(1)}, bf16[128,512]{1,0:T(8,128)(2,1)S(1)}, u32[]{:S(2)}, u32[]{:S(2)}) collective-permute-start(bf16[128,512]{1,0:T(8,128)(2,1)S(1)} %pad_maximum_fusion.1), channel_id=1, source_target_pairs={{0,4},{2,6},{4,0},{6,2},{8,12},{10,14},{12,8},{14,10},{1,5},{3,7},... | collective-permute-start | bytes 393224 | tf_op jit(solution)/shard_map/ppermute | solution.py:335
  14.3 20.7 %collective-permute-start.4 = (bf16[256,512]{1,0:T(8,128)(2,1)S(1)}, bf16[256,512]{1,0:T(8,128)(2,1)S(1)}, u32[]{:S(2)}, u32[]{:S(2)}) collective-permute-start(bf16[256,512]{1,0:T(8,128)(2,1)S(1)} %pad_maximum_fusion.refs_0_), channel_id=1, source_target_pairs={{0,1},{1,0},{2,3},{3,2},{4,5},{5,4},{6,7},{7,6},{8,9},{9,8},{10,11... | collective-permute-start | bytes 786440 | tf_op jit(solution)/shard_map/ppermute | solution.py:338
  14.4 20.6 %collective-permute-start.2 = (bf16[256,512]{1,0:T(8,128)(2,1)S(1)}, bf16[256,512]{1,0:T(8,128)(2,1)S(1)}, u32[]{:S(2)}, u32[]{:S(2)}) collective-permute-start(bf16[256,512]{1,0:T(8,128)(2,1)S(1)} %pad_maximum_fusion.refs_0_), channel_id=1, source_target_pairs={{0,2},{2,0},{4,6},{6,4},{8,10},{10,8},{12,14},{14,12},{1,3},{3,1},... | collective-permute-start | bytes 786440 | tf_op jit(solution)/shard_map/ppermute | solution.py:335
  16.2 1.2 %copy-start = (bf16[16,1,256,128]{3,2,1,0:T(8,128)(2,1)S(1)}, bf16[16,1,256,128]{3,2,1,0:T(8,128)(2,1)}, u32[]{:S(2)}) copy-start(bf16[16,1,256,128]{3,2,1,0:T(8,128)(2,1)} %k_ref.1) | copy-start | bytes 3145732
  17.4 1.2 %copy-start.1 = (bf16[16,1,256,128]{3,2,1,0:T(8,128)(2,1)S(1)}, bf16[16,1,256,128]{3,2,1,0:T(8,128)(2,1)}, u32[]{:S(2)}) copy-start(bf16[16,1,256,128]{3,2,1,0:T(8,128)(2,1)} %v_ref.1) | copy-start | bytes 3145732
  20.9 14.1 %copy-start.2 = (bf16[64,1792]{1,0:T(8,128)(2,1)S(1)}, bf16[64,1792]{1,0:T(8,128)(2,1)}, u32[]{:S(2)}) copy-start(bf16[64,1792]{1,0:T(8,128)(2,1)} %q_ref.4) | copy-start | bytes 688132
  20.9 4.1 %collective-permute-start.5 = (bf16[10,16,128]{2,1,0:T(8,128)(2,1)S(1)}, bf16[10,16,128]{2,1,0:T(8,128)(2,1)S(1)}, u32[]{:S(2)}, u32[]{:S(2)}) collective-permute-start(bf16[10,16,128]{2,1,0:T(8,128)(2,1)S(1)} %decode_local.1.a_ref), channel_id=1, source_target_pairs={{0,4},{2,6},{4,0},{6,2},{8,12},{10,14},{12,8},{14,10},{1,5},{3,7},... | collective-permute-start | bytes 122888 | tf_op jit(solution)/shard_map/ppermute | solution.py:335
  25.1 4.1 %collective-permute-start.6 = (bf16[10,16,128]{2,1,0:T(8,128)(2,1)S(1)}, bf16[10,16,128]{2,1,0:T(8,128)(2,1)S(1)}, u32[]{:S(2)}, u32[]{:S(2)}) collective-permute-start(bf16[10,16,128]{2,1,0:T(8,128)(2,1)S(1)} %decode_merge.3.a_ref), channel_id=1, source_target_pairs={{0,2},{2,0},{4,6},{6,4},{8,10},{10,8},{12,14},{14,12},{1,3},{3,1},... | collective-permute-start | bytes 122888 | tf_op jit(solution)/shard_map/ppermute | solution.py:335
  29.3 5.0 %collective-permute-start.7 = (bf16[10,16,128]{2,1,0:T(8,128)(2,1)S(1)}, bf16[10,16,128]{2,1,0:T(8,128)(2,1)S(1)}, u32[]{:S(2)}, u32[]{:S(2)}) collective-permute-start(bf16[10,16,128]{2,1,0:T(8,128)(2,1)S(1)} %decode_merge.4.a_ref), channel_id=1, source_target_pairs={{0,8},{2,10},{4,12},{6,14},{8,0},{10,2},{12,4},{14,6},{1,9},{3,11}... | collective-permute-start | bytes 122888 | tf_op jit(solution)/shard_map/ppermute | solution.py:335
  32.1 2.9 %copy-start.7 = (s32[16]{0:T(128)S(1)}, s32[16]{0:T(128)}, u32[]{:S(2)}) copy-start(s32[16]{0:T(128)} %span_ref.3) | copy-start | bytes 196
  35.0 1.7 %collective-permute-start.3 = (bf16[256,512]{1,0:T(8,128)(2,1)S(1)}, bf16[256,512]{1,0:T(8,128)(2,1)S(1)}, u32[]{:S(2)}, u32[]{:S(2)}) collective-permute-start(bf16[256,512]{1,0:T(8,128)(2,1)S(1)} %collective-permute-done.2.refs_0_), channel_id=1, source_target_pairs={{0,1},{1,0},{2,3},{3,2},{4,5},{5,4},{6,7},{7,6},{8,9},{9,8},{10,11... | collective-permute-start | bytes 786440 | tf_op jit(solution)/shard_map/ppermute | solution.py:338
